TPU v7x, 32 devices: a whole 2x2x4 slice. The times are simulated.
32 devices in a mesh: sample: 4 (over z), seq: 2 (over core), tensor: 4 (over y, x).
Axes of the slice: x: 2, y: 2, z: 4, core: 2. Of those that a mesh axis runs over, the one named last changes fastest.
Arguments:
- hidden: bfloat16 [4, 256, 4096], P('sample', 'seq'), may hold values from -512 to 512
- weight: bfloat16 [4096, 81920], P(None, ('sample', 'tensor')), may hold values from -1 to 1
- targets: int32 [4, 256], P('sample', 'seq'), may hold values from 0 to 81919
- old_logprob: float32 [4, 256], P('sample', 'seq'), may hold values from -13.65 to -10.65
- lengths: int32 [4], replicated, may hold values from 1 to 256, 640 in all
- group_ids: int32 [4], replicated, may hold values from 0 to 1, as said below
- rewards: int32 [4], P('sample'), may hold values from 0 to 2000
Outputs:
- new_logprob: float32 [4, 256], P('sample', 'seq')
- advantage: float32 [4], P('sample')
- completion_term: float32 [4], P('sample')
- loss: float32 [], replicated
Inputs may be any that keep to these rules, and one draw needn't show every extreme that they name: The lengths sum to 640 and one equals 256. `group_ids`: each prompt id names exactly 2 completions.
All inputs are finite; a program needn't handle non-finite values.
Results may differ from a plain program's by a relative error of at most 0.0003.
Values may be sent and summed in bfloat16 or wider, within the bound.
A program may use at most 128 MiB of HBM per device.

v0:
```python
import jax
import jax.numpy as jnp
from jax import lax
from jax.sharding import PartitionSpec as P

GROUP = 2


CLIP_LOW = 0.8
CLIP_HIGH = 1.28
VAR_FLOOR = 0.25
REWARD_SCALE = 1000.0


def combined_all(value, axis, combine):
    everything = jax.tree.map(lambda part: lax.all_gather(part, axis), value)
    leading = jax.tree.map(lambda part: part[0], everything)

    def lap(k, so_far):
        return combine(so_far, jax.tree.map(lambda part: part[k], everything))

    return lax.fori_loop(1, lax.axis_size(axis), lap, leading)


def combine_stats(former, latter):
    highest = jnp.maximum(former[0], latter[0])
    summed = former[1] * jnp.exp(former[0] - highest) + latter[1] * jnp.exp(latter[0] - highest)
    return (highest, summed, former[2] + latter[2])


def vocab_stats(row_block, weight, token_ids, vocab_start):
    logits = jnp.dot(row_block, weight, preferred_element_type=jnp.float32)
    highest = jnp.max(logits, axis=1)
    summed = jnp.sum(jnp.exp(logits - highest[:, None]), axis=1)
    columns = lax.broadcasted_iota(jnp.int32, logits.shape, 1)
    picked = jnp.sum(
        jnp.where(columns == (token_ids - vocab_start)[:, None], logits, jnp.float32(0.0)), axis=1
    )
    return (highest, summed, picked)


def per_device(hidden, weight, targets, old_logprob, lengths, group_ids, rewards):
    comp_dev, half_len, model_width = hidden.shape
    samples = lax.axis_size("sample")
    vocab_dev = weight.shape[1]
    sample_index = lax.axis_index("sample")
    seq_index = lax.axis_index("seq")
    vocab_start = (sample_index * lax.axis_size("tensor") + lax.axis_index("tensor")) * vocab_dev
    all_targets = lax.all_gather(targets, "sample", axis=0, tiled=True)
    shard_rows = lax.all_gather(hidden, "sample", axis=0, tiled=True)
    piece_rows = shard_rows.shape[0]
    found_stats = vocab_stats(
        shard_rows.reshape(piece_rows * half_len, model_width),
        weight,
        all_targets.reshape(-1),
        vocab_start,
    )
    stacked = jnp.stack(found_stats).reshape(3, piece_rows, half_len)
    highest, summed, picked = (stacked[0], stacked[1], stacked[2])
    shaped = tuple(
        (
            partial_value.reshape(samples, comp_dev, half_len)
            for partial_value in (highest, summed, picked)
        )
    )
    arrived = lax.all_to_all(shaped, "sample", split_axis=0, concat_axis=0, tiled=True)
    peak_value = jnp.max(arrived[0], axis=0)
    local_stats = (
        peak_value,
        jnp.sum(arrived[1] * jnp.exp(arrived[0] - peak_value[None]), axis=0),
        jnp.sum(arrived[2], axis=0),
    )
    highest, summed, picked = combined_all(local_stats, "tensor", combine_stats)
    log_norm = highest + jnp.log(summed)
    own_lengths = lax.dynamic_slice_in_dim(lengths, sample_index * comp_dev, comp_dev, 0)
    own_offsets = seq_index * half_len + lax.broadcasted_iota(jnp.int32, (comp_dev, half_len), 1)
    usable = own_offsets < own_lengths[:, None]
    new_logprob = jnp.where(usable, picked - log_norm, jnp.float32(0.0))
    ratios = jnp.exp(new_logprob - old_logprob)
    clipped = jnp.clip(ratios, CLIP_LOW, CLIP_HIGH)
    reward = rewards.astype(jnp.float32) / REWARD_SCALE
    completions = lengths.shape[0]
    groups = completions // GROUP
    group_range = jnp.arange(groups, dtype=jnp.int32)
    own_groups = lax.dynamic_slice_in_dim(group_ids, sample_index * comp_dev, comp_dev, 0)
    member = (own_groups[:, None] == group_range[None, :]).astype(jnp.float32)
    group_sum, group_square = lax.psum(
        (
            jnp.sum(member * reward[:, None], axis=0),
            jnp.sum(member * (reward * reward)[:, None], axis=0),
        ),
        "sample",
    )
    group_mean = group_sum / GROUP
    group_scale = jnp.sqrt(jnp.maximum(group_square / GROUP - group_mean * group_mean, VAR_FLOOR))
    advantage = (reward - jnp.sum(member * group_mean[None, :], axis=1)) / jnp.sum(
        member * group_scale[None, :], axis=1
    )
    objective = jnp.where(
        usable,
        jnp.minimum(ratios * advantage[:, None], clipped * advantage[:, None]),
        jnp.float32(0.0),
    )
    token_total = lax.psum(jnp.sum(objective, axis=1), "seq")
    completion_term = token_total / own_lengths.astype(jnp.float32)
    loss = -lax.psum(jnp.sum(completion_term), "sample") / completions
    return (new_logprob, advantage, completion_term, loss)


def solution(mesh):
    placed = (
        P("sample", "seq", None),
        P(None, ("sample", "tensor")),
        P("sample", "seq"),
        P("sample", "seq"),
        P(),
        P(),
        P("sample"),
    )
    return jax.shard_map(
        per_device,
        mesh=mesh,
        in_specs=placed,
        out_specs=(P("sample", "seq"), P("sample"), P("sample"), P()),
        check_vma=False,
    )
```

profile of v0, /device:TPU:0, one launch (start us, length us, event | category | flops | bytes accessed | tf_op | source)
XLA Modules:
  0.0 195.8 jit_solution(1551777512251109155)
XLA Ops:
  7.2 0.0 all-gather.9.cloned.1.call-start
  7.2 0.7 all-gather.9.cloned.1.call-update
  8.6 1.2 dynamic_slice.37
  9.8 0.6 fusion.8
  10.4 13.6 %all-reduce = (f32[2]{0:T(128)S(1)}, f32[2]{0:T(128)S(1)}) all-reduce(f32[2]{0:T(128)S(1)} %get-tuple-element.212, f32[2]{0:T(128)S(1)} %get-tuple-element.213), channel_id=1, replica_groups=mesh['sample'=4,'seq'=2,'tensor'=4] {'sample'}, use_global_device_ids=true, to_apply=%region_10.11 | all-reduce | flops 4 | bytes 32 | tf_op jit(solution)/shard_map/psum | solution.py:87
  24.0 1.3 select_reduce_fusion.1
  26.0 1.2 dynamic_slice.36
  28.5 8.1 %all-gather.5 = s32[4,1,128]{2,1,0:T(1,128)S(1)} all-gather(s32[1,1,128]{2,1,0:T(1,128)} %bitcast.57), channel_id=1, replica_groups=mesh['sample'=4,'seq'=2,'tensor'=4] {'sample'}, dimensions={0}, use_global_device_ids=true | all-gather | bytes 2560 | tf_op jit(solution)/shard_map/all_gather | solution.py:49
  36.7 56.4 %all-gather.9.cloned.1.call-done = bf16[4,128,4096]{2,1,0:T(8,128)(2,1)} async-done(((bf16[1,128,4096]{2,1,0:T(8,128)(2,1)}), bf16[4,128,4096]{2,1,0:T(8,128)(2,1)}) %all-gather.9.cloned.1.call-update) | async-done | bytes 4194320 | tf_op jit(solution)/shard_map/all_gather | solution.py:50
  93.1 30.0 %fusion.11 = (f32[512]{0:T(512)}, f32[512,5120]{1,0:T(8,128)}) fusion(bf16[512,4096]{1,0:T(8,128)(2,1)} %bitcast.58, bf16[4096,5120]{1,0:T(8,128)(2,1)} %param.10), kind=kOutput, calls=%fused_computation.27 | convolution fusion | flops 21477457920 | bytes 56625152 | tf_op jit(solution)/shard_map/dot_general | solution.py:32
  123.1 0.0 copy-start
  123.1 3.4 %all-to-all-start = ((f32[4,1,128]{2,1,0:T(1,128)}), f32[4,1,128]{2,1,0:T(1,128)S(1)}, u32[]{:S(2)}, u32[]{:S(2)}) async-start(f32[4,1,128]{2,1,0:T(1,128)} %bitcast.5), calls=%async_computation | async-start | bytes 4096 | tf_op jit(solution)/shard_map/all_to_all | solution.py:66
  126.5 6.4 %select_reduce_fusion = (f32[512]{0:T(512)}, f32[512]{0:T(512)}) fusion(f32[512,5120]{1,0:T(8,128)} %get-tuple-element.211, s32[512]{0:T(512)S(1)} %bitcast.51, f32[512]{0:T(512)} %get-tuple-element.210), kind=kLoop, calls=%fused_computation.10 | loop fusion | flops 13106176 | bytes 10493952 | tf_op jit(solution)/shard_map/reduce_sum | solution.py:36
  132.9 0.0 all-to-all-done
  132.9 5.0 %all-to-all-start.1 = ((f32[4,1,128]{2,1,0:T(1,128)}), f32[4,1,128]{2,1,0:T(1,128)S(1)}, u32[]{:S(2)}, u32[]{:S(2)}) async-start(f32[4,1,128]{2,1,0:T(1,128)} %bitcast.9), calls=%async_computation.1 | async-start | bytes 4096 | tf_op jit(solution)/shard_map/all_to_all | solution.py:66
  137.9 7.9 %all-gather.3 = f32[4,1,128]{2,1,0:T(1,128)S(1)} all-gather(f32[1,1,128]{2,1,0:T(1,128)S(1)} %bitcast.54), channel_id=2, replica_groups=mesh['sample'=4,'seq'=2,'tensor'=4] {'tensor'}, dimensions={0}, use_global_device_ids=true | all-gather | bytes 2560 | tf_op jit(solution)/shard_map/all_gather | solution.py:16
  145.9 0.0 all-to-all-done.1
  145.9 5.1 %all-to-all-start.2 = ((f32[4,1,128]{2,1,0:T(1,128)}), f32[4,1,128]{2,1,0:T(1,128)S(1)}, u32[]{:S(2)}, u32[]{:S(2)}) async-start(f32[4,1,128]{2,1,0:T(1,128)} %bitcast.16), calls=%async_computation.2 | async-start | bytes 4096 | tf_op jit(solution)/shard_map/all_to_all | solution.py:66
  151.0 7.8 %all-gather.4 = f32[4,1,128]{2,1,0:T(1,128)S(1)} all-gather(f32[1,1,128]{2,1,0:T(1,128)S(1)} %bitcast.55), channel_id=3, replica_groups=mesh['sample'=4,'seq'=2,'tensor'=4] {'tensor'}, dimensions={0}, use_global_device_ids=true | all-gather | bytes 2560 | tf_op jit(solution)/shard_map/all_gather | solution.py:16
  158.8 0.0 all-to-all-done.2
  158.8 7.0 %all-gather.6 = f32[4,1,128]{2,1,0:T(1,128)S(1)} all-gather(f32[1,1,128]{2,1,0:T(1,128)S(1)} %bitcast.56), channel_id=4, replica_groups=mesh['sample'=4,'seq'=2,'tensor'=4] {'tensor'}, dimensions={0}, use_global_device_ids=true | all-gather | bytes 2560 | tf_op jit(solution)/shard_map/all_gather | solution.py:16
  165.9 0.1 while.19
  166.0 0.0 copy-done
  166.0 1.8 fusion.7
  167.8 3.1 %psum.30 = f32[1]{0:T(128)} all-reduce(f32[1]{0:T(128)} %bitcast.26), channel_id=1, replica_groups=mesh['sample'=4,'seq'=2,'tensor'=4] {'seq'}, use_global_device_ids=true, to_apply=%region_13.14 | all-reduce | flops 1 | bytes 8 | tf_op jit(solution)/shard_map/psum | solution.py:104
  171.5 13.4 %psum.31 = f32[]{:T(128)} all-reduce(f32[]{:T(128)} %bitcast.27), channel_id=1, replica_groups=mesh['sample'=4,'seq'=2,'tensor'=4] {'sample'}, use_global_device_ids=true, to_apply=%region_14.15 | all-reduce | flops 1 | bytes 8 | tf_op jit(solution)/shard_map/psum | solution.py:106
  (10 shorter events, 0.1 us)
Async XLA Ops:
  7.2 85.9 %all-gather.9.cloned.1.call-start = ((), (), s32[]{:S(2)}) async-start(), calls=%async_computation.3 | async-start | bytes 5242880 | tf_op jit(solution)/shard_map/all_gather | solution.py:50
  123.1 42.9 %copy-start = (f32[1,128]{1,0:T(1,128)S(1)}, f32[1,128]{1,0:T(1,128)}, u32[]{:S(2)}) copy-start(f32[1,128]{1,0:T(1,128)} %param.12) | copy-start | bytes 1540
  123.1 9.7 %all-to-all-start = ((f32[4,1,128]{2,1,0:T(1,128)}), f32[4,1,128]{2,1,0:T(1,128)S(1)}, u32[]{:S(2)}, u32[]{:S(2)}) async-start(f32[4,1,128]{2,1,0:T(1,128)} %bitcast.5), calls=%async_computation | async-start | bytes 4096 | tf_op jit(solution)/shard_map/all_to_all | solution.py:66
  132.9 13.0 %all-to-all-start.1 = ((f32[4,1,128]{2,1,0:T(1,128)}), f32[4,1,128]{2,1,0:T(1,128)S(1)}, u32[]{:S(2)}, u32[]{:S(2)}) async-start(f32[4,1,128]{2,1,0:T(1,128)} %bitcast.9), calls=%async_computation.1 | async-start | bytes 4096 | tf_op jit(solution)/shard_map/all_to_all | solution.py:66
  145.9 13.0 %all-to-all-start.2 = ((f32[4,1,128]{2,1,0:T(1,128)}), f32[4,1,128]{2,1,0:T(1,128)S(1)}, u32[]{:S(2)}, u32[]{:S(2)}) async-start(f32[4,1,128]{2,1,0:T(1,128)} %bitcast.16), calls=%async_computation.2 | async-start | bytes 4096 | tf_op jit(solution)/shard_map/all_to_all | solution.py:66
Sparse Core Ops, SparseCore 0:
  9.5 83.5 all-gather.8
where the time goes:
time: 196 us
  blocking collectives  61 us (31%)
  waiting for transfers between devices  57.1 us (29%)
  matrix products  30 us (15%)
  between operations  21.4 us (11%)
  starting transfers between devices  13.5 us (7%)
  other arithmetic  10.2 us (5%)
  local copies, waits for them, and re-layouts  2.49 us (1%)
    all_gather x1, waiting for transfers between devices, per_device(): shard_rows = lax.all_gather(hidden, 'sample', axis=0, tiled=True)  56.4 us
    dot_general x1, matrix products, vocab_stats(): logits = jnp.dot(row_block, weight, preferred_element_type=jnp.float32)  30 us
    all_gather x3, blocking collectives, combined_all(): everything = jax.tree.map(lambda part: lax.all_gather(part, axis), value)  22.8 us
    psum x1, blocking collectives, per_device(): lax.psum((jnp.sum(member * reward[:, None], axis=0), jnp.sum(member * (re...  13.6 us
    all_to_all x3, starting transfers between devices, per_device(): lax.all_to_all(shaped, 'sample', split_axis=0, concat_axis=0, tiled=True)  13.5 us
    psum x1, blocking collectives, per_device(): loss = -lax.psum(jnp.sum(completion_term), 'sample') / completions  13.4 us
    all_gather x1, blocking collectives, per_device(): all_targets = lax.all_gather(targets, 'sample', axis=0, tiled=True)  8.14 us
    reduce_sum x1, other arithmetic, vocab_stats(): jnp.sum(jnp.where(columns == (token_ids - vocab_start)[:, None], logits,...  6.36 us
  transfers between devices with their start and end apart: 4, of which 1 were waited for; matrix products, arithmetic and copies ran while one was open for 6% of the time, Pallas kernels for 0%

commit v1 on v0

v1 whole, which is shorter than its diff:
```python
import functools

import jax
import jax.numpy as jnp
from jax import lax
from jax.experimental import pallas as pl
from jax.experimental.pallas import tpu as pltpu
from jax.sharding import PartitionSpec as P

GROUP = 2


CLIP_LOW = 0.8
CLIP_HIGH = 1.28
VAR_FLOOR = 0.25
REWARD_SCALE = 1000.0
LANES = 128
MESH = pl.DeviceIdType.MESH
Z, X, Y, DX, DY, CZ, CX, CY, CD = range(9)


def not_negative(value, bound):
    return lax.div(value + bound, bound)


def merge(stats):
    highest = functools.reduce(jnp.maximum, [s[0:1] for s in stats])
    summed = sum(s[1:2] * jnp.exp(s[0:1] - highest) for s in stats)
    picked = sum(s[2:3] for s in stats)
    return highest, summed, picked


def store_stats(ref, highest, summed, picked):
    ref[0:1, :] = highest
    ref[1:2, :] = summed
    ref[2:3, :] = picked


def kernel(
    sizes,
    hidden_ref,
    weight_ref,
    aux_ref,
    length_ref,
    same_ref,
    out_ref,
    rows,
    w,
    aux,
    run,
    stat,
    arrived_a,
    joined,
    arrived_b,
    term,
    arrived_c,
    send,
    recv,
    own_sem,
    w_sem,
    aux_send,
    aux_recv,
    a_send,
    a_recv,
    b_send,
    b_recv,
    c_send,
    c_recv,
):
    samples, tensors, half, tiles, tile = sizes
    s = lax.axis_index("sample")
    c = lax.axis_index("seq")
    t = lax.axis_index("tensor")
    other = 1 - c
    x_near = t + 1 - 2 * lax.rem(t, 2)
    y_near = t + 2 - 4 * lax.div(t, 2)
    unit = half // tensors
    part = unit // 2
    local = pltpu.make_async_copy(
        hidden_ref, rows.at[s, pl.ds(pl.multiple_of(c * half, half), half)], own_sem.at[0]
    )
    local.start()
    width = tiles * tile

    def weight_copy(i):
        first = pl.multiple_of(c * width + i * tile, LANES)
        return pltpu.make_async_copy(weight_ref.at[:, pl.ds(first, tile)], w.at[i], w_sem.at[i])

    for i in range(tiles):
        weight_copy(i).start()

    def at_column(k):
        return {"sample": lax.rem(s + k // 2, samples), "seq": lax.rem(c + k % 2, 2)}

    def in_plane(k):
        return {"seq": lax.rem(c + k % 2, 2), "tensor": lax.rem(t + k // 2, tensors)}

    barrier = pltpu.get_barrier_semaphore()
    for k in range(1, 2 * samples):
        pl.semaphore_signal(barrier, inc=1, device_id=at_column(k), device_id_type=MESH)
    for k in range(2, 2 * tensors):
        pl.semaphore_signal(barrier, inc=1, device_id=in_plane(k), device_id_type=MESH)
    pl.semaphore_wait(barrier, 2 * samples - 1 + 2 * tensors - 2)

    def remote(src, dst, send_sem, recv_sem, device):
        return pltpu.make_async_remote_copy(
            src_ref=src,
            dst_ref=dst,
            send_sem=send_sem,
            recv_sem=recv_sem,
            device_id=device,
            device_id_type=MESH,
        )

    def piece(plane, core, owner, shift, count):
        return rows.at[plane, pl.ds(pl.multiple_of(core * half + owner * unit + shift, 16), count)]

    def moved(kind, plane, owner, shift, count, device):
        ref = piece(plane, c, owner, shift, count)
        return remote(ref, ref, send.at[kind, plane], recv.at[kind, plane], device)

    def awaited(kind, plane, core, owner, shift, count):
        ref = piece(plane, core, owner, shift, count)
        remote(ref, ref, send.at[kind, plane], recv.at[kind, plane], {"seq": other}).wait_recv()

    local.wait()
    own_unit = piece(s, c, t, 0, unit)
    own_rows = rows.at[s, pl.ds(pl.multiple_of(c * half, half), half)]
    to_right = remote(own_unit, own_unit, own_sem.at[1], recv.at[Z, s], {"sample": lax.rem(s + 1, samples)})
    to_left = remote(
        own_unit, own_unit, own_sem.at[2], recv.at[Z, s], {"sample": lax.rem(s + samples - 1, samples)}
    )
    to_core = remote(own_rows, own_rows, own_sem.at[3], recv.at[CZ, s], {"seq": other})
    pl.when(s < samples - 1)(to_right.start)
    pl.when(s > 0)(to_left.start)

    def aux_copy(k):
        return remote(
            aux_ref, aux.at[2 * s + c], aux_send.at[k], aux_recv.at[2 * s + c], at_column(k)
        )

    for k in range(1, 2 * samples):
        aux_copy(k).start()
    to_core.start()
    aux[2 * s + c] = aux_ref[...]
    for k in range(1, 2 * samples):
        source = 2 * lax.rem(s + k // 2, samples) + lax.rem(c + k % 2, 2)
        remote(aux_ref, aux.at[source], aux_send.at[k], aux_recv.at[source], {"seq": other}).wait_recv()

    pairs = jnp.minimum(s, samples - 1 - s)
    rightward = not_negative(samples - 1 - 2 * s, 2 * samples)

    def plane_of(j):
        if j == 0:
            return s
        single = not_negative(j - 2 * pairs - 1, 2 * samples)
        paired = s + (j + 1) // 2 * (1 if j % 2 else -1)
        alone = s + (2 * rightward - 1) * (j - pairs)
        return paired + single * (alone - paired)

    planes = [plane_of(j) for j in range(samples)]

    def onward(p):
        from_left = not_negative(s - p, 2 * samples)
        nxt = s + 2 * from_left - 1
        inside = (nxt >= 0) & (nxt < samples)
        copy = moved(Z, p, t, 0, unit, {"sample": lax.rem(nxt + samples, samples)})
        return inside, copy

    def sends(j):
        p = planes[j]
        return {
            X: lambda: moved(X, p, t, 0, unit, {"tensor": x_near}),
            Y: lambda: moved(Y, p, t, 0, unit, {"tensor": y_near}),
            CZ: lambda: moved(CZ, p, t, 0, unit, {"seq": other}),
            DY: lambda: moved(DY, p, x_near, 0, part, {"tensor": y_near}),
            CX: lambda: moved(CX, p, x_near, 0, unit, {"seq": other}),
            DX: lambda: moved(DX, p, y_near, part, part, {"tensor": x_near}),
            CY: lambda: moved(CY, p, y_near, 0, unit, {"seq": other}),
            CD: lambda: moved(CD, p, tensors - 1 - t, 0, unit, {"seq": other}),
        }

    def event_z(j):
        p = planes[j]
        awaited(Z, p, c, t, 0, unit)
        inside, copy = onward(p)
        pl.when(inside)(copy.start)
        out = sends(j)
        out[X]().start()
        out[Y]().start()
        out[CZ]().start()

    def event_xy(j):
        p = planes[j]
        out = sends(j)
        awaited(X, p, c, x_near, 0, unit)
        out[DY]().start()
        out[CX]().start()
        awaited(Y, p, c, y_near, 0, unit)
        out[DX]().start()
        out[CY]().start()

    def event_d(j):
        p = planes[j]
        far = tensors - 1 - t
        awaited(DY, p, c, far, 0, part)
        awaited(DX, p, c, far, part, part)
        sends(j)[CD]().start()

    def from_core(j):
        p = planes[j]
        if j == 0:
            block = rows.at[p, pl.ds(pl.multiple_of(other * half, half), half)]
            remote(block, block, own_sem.at[3], recv.at[CZ, p], {"seq": other}).wait_recv()
            return
        awaited(CZ, p, other, t, 0, unit)
        awaited(CX, p, other, x_near, 0, unit)
        awaited(CY, p, other, y_near, 0, unit)
        awaited(CD, p, other, tensors - 1 - t, 0, unit)

    slice_start = ((s * tensors + t) * 2 + c) * width

    def begin(j):
        from_core(j)
        p = planes[j]
        run[0] = jnp.full((2 * half, LANES), -jnp.inf, jnp.float32)
        run[1] = jnp.zeros((2 * half, LANES), jnp.float32)
        run[2] = jnp.zeros((2 * half, LANES), jnp.float32)
        for h in range(2):
            ids = jnp.broadcast_to(aux[2 * p + h][2:3, :], (LANES, half))
            run[3, h * half : (h + 1) * half, :] = ids.T

    def compute(j, first, last):
        p = planes[j]

        def step(i, carry):
            if j == 0:
                weight_copy(i).wait()
            logits = jnp.dot(rows[p], w[i], preferred_element_type=jnp.float32)
            chunks = [logits[:, k : k + LANES] for k in range(0, tile, LANES)]
            before = run[0]
            highest = functools.reduce(jnp.maximum, chunks, before)
            run[0] = highest
            run[1] = run[1] * jnp.exp(before - highest) + sum(jnp.exp(x - highest) for x in chunks)
            lane = lax.broadcasted_iota(jnp.int32, (2 * half, LANES), 1)
            wanted = run[3].astype(jnp.int32) - (slice_start + i * tile)
            run[2] += sum(
                jnp.where(lane + k * LANES == wanted, x, jnp.float32(0.0)) for k, x in enumerate(chunks)
            )
            return carry

        lax.fori_loop(first, last, step, 0)

    def finish(j):
        p = planes[j]
        highest = run[0].T
        top = jnp.max(highest, axis=0, keepdims=True)
        summed = jnp.sum(run[1].T * jnp.exp(highest - top), axis=0, keepdims=True)
        picked = jnp.sum(run[2].T, axis=0, keepdims=True)
        store_stats(stat.at[p], top, summed, picked)
        if j:
            stage_a(j).start()

    def stage_a(j):
        p = planes[j]
        return remote(stat.at[p], arrived_a.at[s], a_send.at[p], a_recv.at[s], {"sample": p})

    begin(0)
    compute(0, 0, tiles)
    finish(0)
    event_z(1)
    cut = tiles // 2
    for j in range(1, samples):
        if j + 1 < samples:
            event_z(j + 1)
        if j >= 2:
            begin(j - 1)
            compute(j - 1, 0, cut)
        event_xy(j)
        if j >= 2:
            compute(j - 1, cut, tiles)
            finish(j - 1)
        event_d(j)
    begin(samples - 1)
    compute(samples - 1, 0, tiles)
    finish(samples - 1)

    group_sum = jnp.zeros((1, LANES), jnp.float32)
    group_square = jnp.zeros((1, LANES), jnp.float32)
    for p in range(samples):
        reward = aux[2 * p][1:2, :]
        group_sum += same_ref[p : p + 1, :] * reward
        group_square += same_ref[p : p + 1, :] * (reward * reward)
    group_mean = group_sum / GROUP
    group_scale = jnp.sqrt(jnp.maximum(group_square / GROUP - group_mean * group_mean, VAR_FLOOR))
    advantage = (aux_ref[1:2, :] - group_mean) / group_scale

    collected = [stat[s]]
    for k in range(1, samples):
        source = lax.rem(s + k, samples)
        remote(stat.at[s], arrived_a.at[source], a_send.at[source], a_recv.at[source], {"sample": source}).wait_recv()
        collected.append(arrived_a[source])
    store_stats(joined, *merge(collected))

    def stage_b(k):
        here = 2 * t + c
        return remote(joined, arrived_b.at[here], b_send.at[k], b_recv.at[here], in_plane(k))

    for k in range(1, 2 * tensors):
        stage_b(k).start()
    collected = [joined[...]]
    for k in range(1, 2 * tensors):
        source = 2 * lax.rem(t + k // 2, tensors) + lax.rem(c + k % 2, 2)
        remote(joined, arrived_b.at[source], b_send.at[k], b_recv.at[source], {"seq": other}).wait_recv()
        collected.append(arrived_b[source])
    highest, summed, picked = merge(collected)
    logprob = picked - (highest + jnp.log(summed))
    total = jnp.zeros((1, 1), jnp.float32)
    halves = []
    length = length_ref[0:1, :]
    for h in range(2):
        position = h * half + lax.broadcasted_iota(jnp.int32, (1, half), 1)
        usable = position.astype(jnp.float32) < length
        new = jnp.where(usable, logprob[:, h * half : (h + 1) * half], jnp.float32(0.0))
        halves.append(new)
        ratios = jnp.exp(new - aux[2 * s + h][0:1, :])
        clipped = jnp.clip(ratios, CLIP_LOW, CLIP_HIGH)
        objective = jnp.where(
            usable, jnp.minimum(ratios * advantage, clipped * advantage), jnp.float32(0.0)
        )
        total += jnp.sum(objective, axis=1, keepdims=True)
    own_term = jnp.broadcast_to(total, (1, LANES)) / length
    term[...] = jnp.broadcast_to(own_term, term.shape)

    def stage_c(k):
        return remote(
            term, arrived_c.at[s], c_send.at[k], c_recv.at[s], {"sample": lax.rem(s + k, samples)}
        )

    for k in range(1, samples):
        stage_c(k).start()
    mine = c.astype(jnp.float32)
    out_ref[0:1, :] = halves[0] * (1.0 - mine) + halves[1] * mine
    out_ref[1:2, :] = advantage
    out_ref[2:3, :] = own_term
    loss = own_term
    for k in range(1, samples):
        source = lax.rem(s + k, samples)
        remote(term, arrived_c.at[source], c_send.at[k], c_recv.at[source], {"seq": other}).wait_recv()
    arrived_c[s] = term[...]
    loss = sum(arrived_c[p][0:1, :] for p in range(samples))
    out_ref[3:4, :] = -loss / samples
    out_ref[4:8, :] = jnp.zeros((4, LANES), jnp.float32)

    pl.when(s < samples - 1)(to_right.wait_send)
    pl.when(s > 0)(to_left.wait_send)
    to_core.wait_send()
    for k in range(1, 2 * samples):
        aux_copy(k).wait_send()
    for j in range(1, samples):
        inside, copy = onward(planes[j])
        pl.when(inside)(copy.wait_send)
        for copy in sends(j).values():
            copy().wait_send()
        stage_a(j).wait_send()
        stage_c(j).wait_send()
    for k in range(1, 2 * tensors):
        stage_b(k).wait_send()


def per_device(hidden, weight, targets, old_logprob, lengths, group_ids, rewards):
    _, half, model_width = hidden.shape
    samples = lax.axis_size("sample")
    tensors = lax.axis_size("tensor")
    width = weight.shape[1] // 2
    tile = max(n for n in range(LANES, 513, LANES) if width % n == 0)
    tiles = width // tile
    s = lax.axis_index("sample")
    reward = rewards.astype(jnp.float32) / REWARD_SCALE
    aux = jnp.concatenate(
        [
            old_logprob,
            jnp.broadcast_to(reward[:, None], (1, half)),
            targets.astype(jnp.float32),
            jnp.zeros((5, half), jnp.float32),
        ]
    )
    own_length = lax.dynamic_slice_in_dim(lengths, s, 1).astype(jnp.float32)
    own_group = lax.dynamic_slice_in_dim(group_ids, s, 1)
    length = jnp.broadcast_to(own_length[:, None], (8, LANES))
    same = jnp.broadcast_to((group_ids == own_group).astype(jnp.float32)[:, None], (samples, LANES))
    f32 = jnp.float32
    dma = pltpu.SemaphoreType.DMA
    vmem = pl.BlockSpec(memory_space=pltpu.VMEM)
    out = pl.pallas_call(
        functools.partial(kernel, (samples, tensors, half, tiles, tile)),
        out_shape=jax.ShapeDtypeStruct((8, LANES), f32),
        in_specs=[
            pl.BlockSpec(memory_space=pltpu.HBM),
            pl.BlockSpec(memory_space=pltpu.HBM),
            vmem,
            vmem,
            vmem,
        ],
        out_specs=vmem,
        scratch_shapes=[
            pltpu.VMEM((samples, 2 * half, model_width), jnp.bfloat16),
            pltpu.VMEM((tiles, model_width, tile), jnp.bfloat16),
            pltpu.VMEM((2 * samples, 8, half), f32),
            pltpu.VMEM((4, 2 * half, LANES), f32),
            pltpu.VMEM((samples, 8, 2 * half), f32),
            pltpu.VMEM((samples, 8, 2 * half), f32),
            pltpu.VMEM((8, 2 * half), f32),
            pltpu.VMEM((2 * tensors, 8, 2 * half), f32),
            pltpu.VMEM((8, LANES), f32),
            pltpu.VMEM((samples, 8, LANES), f32),
            dma((9, samples)),
            dma((9, samples)),
            dma((4,)),
            dma((tiles,)),
            dma((2 * samples,)),
            dma((2 * samples,)),
            dma((samples,)),
            dma((samples,)),
            dma((2 * tensors,)),
            dma((2 * tensors,)),
            dma((samples,)),
            dma((samples,)),
        ],
        compiler_params=pltpu.CompilerParams(
            collective_id=0, has_side_effects=True, vmem_limit_bytes=60 * 1024 * 1024
        ),
    )(hidden.reshape(half, model_width), weight, aux, length, same)
    return (out[0:1], out[1, 0:1], out[2, 0:1], out[3, 0])


def solution(mesh):
    placed = (
        P("sample", "seq", None),
        P(None, ("sample", "tensor")),
        P("sample", "seq"),
        P("sample", "seq"),
        P(),
        P(),
        P("sample"),
    )
    return jax.shard_map(
        per_device,
        mesh=mesh,
        in_specs=placed,
        out_specs=(P("sample", "seq"), P("sample"), P("sample"), P()),
        check_vma=False,
    )
```

time: 196 us -> 99.4 us (0.51)
  Pallas kernels: 0 us -> 87.5 us
  blocking collectives: 61 us -> 0 us
  waiting for transfers between devices: 57.1 us -> 0 us
  matrix products: 30 us -> 0 us
  between operations: 21.4 us -> 1.95 us
  starting transfers between devices: 13.5 us -> 0 us
  other arithmetic: 10.2 us -> 3.27 us
  local copies, waits for them, and re-layouts: 2.49 us -> 6.36 us
    pallas_call x0 -> x1, Pallas kernels: none -> 87.5 us  [per_device(): pl.pallas_call(functools.partial(kernel, (samples, tensors, half, tiles,...]
    all_gather x1 -> x0, waiting for transfers between devices: 56.4 us -> none  [per_device(): shard_rows = lax.all_gather(hidden, 'sample', axis=0, tiled=True)]
    all_gather x4 -> x0, blocking collectives: 30.9 us -> none  [the longest x3 22.8 us: combined_all(): everything = jax.tree.map(lambda part: lax.all_gather(part, axis), value)]
    dot_general x1 -> x0, matrix products: 30 us -> none  [vocab_stats(): logits = jnp.dot(row_block, weight, preferred_element_type=jnp.float32)]
    psum x3 -> x0, blocking collectives: 30 us -> none  [the longest x1 13.6 us: per_device(): lax.psum((jnp.sum(member * reward[:, None], axis=0), jnp.sum(member * (re...]
    all_to_all x3 -> x0, starting transfers between devices: 13.5 us -> none  [per_device(): lax.all_to_all(shaped, 'sample', split_axis=0, concat_axis=0, tiled=True)]
    reduce_sum x5 -> x0, other arithmetic: 9.43 us -> none  [the longest x1 6.36 us: vocab_stats(): jnp.sum(jnp.where(columns == (token_ids - vocab_start)[:, None], logits,...]
    slice x0 -> x2, local copies, waits for them, and re-layouts: none -> 2.5 us  [per_device(): return (out[0:1], out[1, 0:1], out[2, 0:1], out[3, 0])]
  transfers between devices with their start and end apart: 4 -> 0, of which waited for: 1 -> 0; matrix products, arithmetic and copies ran while one was open for 6% -> 0% of each run, Pallas kernels for 0% -> 0%
where the time goes in v1:
time: 99.4 us; the launch traced here: 99.1 us
  Pallas kernels  87.5 us (88%)
  local copies, waits for them, and re-layouts  6.36 us (6%)
  other arithmetic  3.27 us (3%)
  between operations  1.95 us (2%)
    pallas_call x1, Pallas kernels, per_device(): pl.pallas_call(functools.partial(kernel, (samples, tensors, half, tiles,...  87.5 us
    slice x2, local copies, waits for them, and re-layouts, per_device(): return (out[0:1], out[1, 0:1], out[2, 0:1], out[3, 0])  2.5 us

profile of v1, /device:TPU:0, one launch (start us, length us, event | category | flops | bytes accessed | tf_op | source)
XLA Modules:
  0.0 99.1 jit_solution(17261215704558521749)
XLA Ops:
  1.3 1.2 %dynamic_slice.7 = s32[1]{0:T(128)} dynamic-slice(s32[4]{0:T(128)} %param.12, s32[]{:T(128)S(6)} %select_n.4), dynamic_slice_sizes={1} | dynamic-slice | bytes 12 | tf_op jit(solution)/shard_map/dynamic_slice | solution.py:389
  2.5 1.3 %compare_convert_fusion = f32[4]{0:T(128)S(1)} fusion(s32[4]{0:T(128)} %param.12, s32[]{:T(128)} %bitcast.3), kind=kLoop, calls=%fused_computation.1 | loop fusion | flops 8 | bytes 36 | tf_op jit(solution)/shard_map/convert_element_type | solution.py:391
  3.8 0.1 pad.1.clone
  3.9 1.2 %dynamic_slice.6 = s32[1]{0:T(128)} dynamic-slice(s32[4]{0:T(128)} %param.11, s32[]{:T(128)S(6)} %select_n.4), dynamic_slice_sizes={1} | dynamic-slice | bytes 12 | tf_op jit(solution)/shard_map/dynamic_slice | solution.py:388
  5.8 0.7 convert_element_type.13
  6.5 0.1 pad.3.clone
  6.5 0.6 broadcast_in_dim.30.same_ref
  7.2 1.3 %maximum_maximum_fusion.aux_ref = f32[8,128]{1,0:T(8,128)} fusion(f32[1,128]{1,0:T(1,128)S(1)} %convert_element_type.13, f32[1,128]{1,0:T(1,128)} %param.10, f32[8]{0:T(128)S(1)} %pad.3.clone, f32[8]{0:T(128)S(1)} %pad.1.clone), kind=kLoop, calls=%fused_computation | loop fusion | flops 3072 | bytes 5184 | tf_op jit(solution)/shard_map/concatenate | solution.py:380
  8.5 0.6 broadcast_in_dim.29.length_ref
  9.1 87.5 %shard_map.102 = f32[8,128]{1,0:T(8,128)} custom-call(bf16[128,4096]{1,0:T(8,128)(2,1)} %bitcast.7, bf16[4096,5120]{1,0:T(8,128)(2,1)} %weight_ref.1, f32[8,128]{1,0:T(8,128)} %maximum_maximum_fusion.aux_ref, f32[8,128]{1,0:T(8,128)} %broadcast_in_dim.29.length_ref, f32[4,128]{1,0:T(4,128)} %broadcast_in_dim.30.same_ref), custom_call_target="tpu_custom_call" | custom-call | tf_op jit(solution)/shard_map/pallas_call | solution.py:395
  96.6 1.2 %slice.12 = f32[1,128]{1,0:T(1,128)} slice(f32[8,128]{1,0:T(8,128)} %shard_map.102), slice={[0:1], [0:128]} | slice | bytes 1024 | tf_op jit(solution)/shard_map/slice | solution.py:434
  97.8 1.3 %fusion = (f32[1,1]{1,0:T(1,128)}, f32[1,1]{1,0:T(1,128)}, f32[1,1]{1,0:T(1,128)}) fusion(f32[8,128]{1,0:T(8,128)} %shard_map.102), kind=kLoop, calls=%fused_computation.2 | loop fusion | bytes 24 | tf_op jit(solution)/shard_map/slice | solution.py:434
  (1 shorter events, 0.0 us)
